TPU v7x, 256 devices: a whole 4x4x8 slice. The times are simulated.
256 devices in a mesh: dp: 4 (over x), expert: 64 (over z, y, core).
Axes of the slice: x: 4, y: 4, z: 8, core: 2. Of those that a mesh axis runs over, the one named last changes fastest.
Arguments:
- rollout_states: bfloat16 [64, 32, 2, 4096], P('expert', 'dp'), may hold values from -30 to 30
- lengths: int32 [32], P('dp'), may hold values from 8 to 128
- group_ids: int32 [32], P('dp'), may hold values from 0 to 3, as said below
- route_ids: int32 [64, 32, 2, 8], P('expert', 'dp'), may hold values from 0 to 63, all different within a row; in each aligned block of 16 rows (0 to 15, 16 to 31, ..., all dimensions but the last counted through in order) at most 4 rows name the same one
- route_weights: float32 [64, 32, 2, 8], P('expert', 'dp'), may hold values from 0.05 to 0.4
- gain_in: float32 [4096], replicated, may hold values from 0.5 to 1.5
- w_gate: bfloat16 [64, 4096, 1024], P('expert', None, 'dp'), may hold values from -0.09375 to 0.09375
- w_up: bfloat16 [64, 4096, 1024], P('expert', None, 'dp'), may hold values from -0.09375 to 0.09375
- w_down: bfloat16 [64, 1024, 4096], P('expert', 'dp'), may hold values from -0.1875 to 0.1875
- gain_out: float32 [4096], replicated, may hold values from 0.5 to 1.5
- head_weight: bfloat16 [4096, 65536], P(None, 'expert'), may hold values from -16 to 16
- targets: int32 [64, 32, 2], P('expert', 'dp'), may hold values from 0 to 65535
- policy_logp: float32 [64, 32, 2], P('expert', 'dp'), may hold values from -14 to -6
Outputs:
- token_kl: float32 [64, 32, 2], P('expert', 'dp')
- row_kl: float32 [32], P('dp')
Inputs may be any that keep to these rules, and one draw needn't show every extreme that they name: `group_ids`: every prompt group has exactly 8 rows; group g is owned by index g mod 4 of dp, so every index owns exactly 8 rows. `route_ids`: every token names 8 different experts. Among the 16 tokens of one device no expert is named more than 4 times, and that bound is reached in every draw.
All inputs are finite; a program needn't handle non-finite values.
Results may differ from a plain program's by a relative error of at most 0.0055.
Values may be sent and summed in bfloat16 or wider, within the bound.
No kernel may reach another device: no remote copies, remote signals or barrier semaphores. Data moves between devices by JAX's collectives and lax.ppermute only.
A program may use at most 192 MiB of HBM per device.

v0:
```python
import jax
import jax.numpy as jnp
from jax import lax
from jax.sharding import PartitionSpec as P


def laid_out(blocks, dim):
    dims = list(blocks.shape[1:])
    dims[dim] *= blocks.shape[0]
    return jnp.moveaxis(blocks, 0, dim).reshape(dims)


def sent_to_all(value, axis):
    copies = jnp.broadcast_to(value, (lax.axis_size(axis), *value.shape))
    return lax.all_to_all(copies, axis, split_axis=0, concat_axis=0, tiled=True)


def gather_directly(value, axis, dim):
    return laid_out(sent_to_all(value, axis), dim)


def gather_turned(arrays, axis, dims):
    turned = [jnp.moveaxis(a, dim, 0) for a, dim in zip(arrays, dims)]
    both = jnp.concatenate([t.reshape(len(t), -1) for t in turned], axis=1)
    whole, at, done = (lax.all_gather(both, axis, axis=0, tiled=True), 0, [])
    for t, dim in zip(turned, dims):
        share = whole[:, at : at + t[0].size].reshape(-1, *t.shape[1:])
        done.append(jnp.moveaxis(share, 0, dim))
        at += t[0].size
    return tuple(done)


def sent_together(arrays, axis, split_dim, concat_dim, along):
    widths = [a.shape[along] for a in arrays]
    both = jnp.concatenate(arrays, axis=along)
    whole = lax.all_to_all(both, axis, split_axis=split_dim, concat_axis=concat_dim, tiled=True)
    return tuple(jnp.split(whole, [sum(widths[:k]) for k in range(1, len(widths))], axis=along))


def taken_together(value, axis):
    return sent_to_all(value, axis).sum(axis=0)


def scaled_norm(values, gain_vec):
    mean_square = jnp.mean(values * values, axis=-1, keepdims=True)
    return values * lax.rsqrt(mean_square + 1e-06) * gain_vec


def expert_mlp(slot_input, gate_part, up_part, down_part):
    gate_act = jnp.dot(slot_input, gate_part, preferred_element_type=jnp.float32)
    up_act = jnp.dot(slot_input, up_part, preferred_element_type=jnp.float32)
    hidden = (jax.nn.silu(gate_act) * up_act).astype(jnp.bfloat16)
    return jnp.dot(hidden, down_part, preferred_element_type=jnp.float32)


def first_ranks(member):
    return jnp.sum((jnp.cumsum(member, axis=0) - member) * member, axis=1)


def on_device(
    rollout_states,
    lengths,
    group_ids,
    route_ids,
    route_weights,
    gain_in,
    w_gate,
    w_up,
    w_down,
    gain_out,
    head_weight,
    targets,
    policy_logp,
):
    owners = lax.axis_size("dp")
    own_owner = lax.axis_index("dp")
    row_count = group_ids.shape[0]
    states_rows = rollout_states[0]
    row_shape = states_rows.shape[1:]
    owner_range = jnp.arange(owners, dtype=jnp.int32)
    all_states, all_groups, all_lengths = (
        gather_directly(rollout_states, "dp", 1),
        gather_directly(group_ids, "dp", 0),
        gather_directly(lengths, "dp", 0),
    )
    all_owner = all_groups % owners
    member = (all_owner[:, None] == owner_range[None, :]).astype(jnp.int32)
    global_rank = first_ranks(member)
    arrival = jnp.where(all_owner == own_owner, global_rank, row_count)
    arrived_states = all_states[0]
    owned_rows = jnp.zeros_like(states_rows).at[arrival].set(arrived_states, mode="drop")
    owned_lengths = jnp.zeros((row_count,), jnp.int32).at[arrival].set(all_lengths, mode="drop")
    features = row_shape[1]
    pos_count = row_shape[0]
    states_flat = owned_rows.reshape(-1, features)
    token_count = states_flat.shape[0]
    expert_ids = route_ids.reshape(token_count, -1)
    gate_values = route_weights.reshape(token_count, -1)
    topk_count = expert_ids.shape[1]
    experts = lax.axis_size("expert")
    slot_bound = min(token_count, 2 * token_count * topk_count // experts)
    states_wide = states_flat.astype(jnp.float32)
    normed_in = scaled_norm(states_wide, gain_in).astype(jnp.bfloat16)
    flat_ids = expert_ids.reshape(-1)
    member_slots = (flat_ids[:, None] == jnp.arange(experts, dtype=jnp.int32)[None, :]).astype(
        jnp.int32
    )
    slot_index = flat_ids * slot_bound + first_ranks(member_slots)
    token_of = jnp.arange(flat_ids.shape[0], dtype=jnp.int32) // topk_count
    sender = (
        jnp.zeros((experts * slot_bound, features), jnp.bfloat16)
        .at[slot_index]
        .set(normed_in[token_of])
    )
    gate_full, up_full, down_full = gather_turned((w_gate, w_up, w_down), "dp", (2, 2, 1))
    arrived = lax.all_to_all(
        sender.reshape(experts, slot_bound, features),
        "expert",
        split_axis=0,
        concat_axis=0,
        tiled=True,
    )
    slot_input = arrived.reshape(-1, features)
    result = expert_mlp(slot_input, gate_full[0], up_full[0], down_full[0])
    worked = result.astype(jnp.bfloat16).reshape(arrived.shape)
    returned = lax.all_to_all(worked, "expert", split_axis=0, concat_axis=0, tiled=True)
    picked = returned.reshape(-1, features)[slot_index].reshape(token_count, topk_count, features)
    routed = jnp.sum(gate_values[:, :, None] * picked.astype(jnp.float32), axis=1)
    mixed_sum = states_wide + routed
    final_rows = scaled_norm(mixed_sum, gain_out).astype(jnp.bfloat16)
    vocab_part = head_weight.shape[1]
    vocab_start = lax.axis_index("expert") * vocab_part
    flat_targets = targets.reshape(-1)
    piece_rows = lax.all_gather(final_rows, "expert", axis=0, tiled=True)
    piece_targets = lax.all_gather(flat_targets, "expert", axis=0, tiled=True)
    logits = jnp.dot(piece_rows, head_weight, preferred_element_type=jnp.float32)
    peak_value = jnp.max(logits, axis=1)
    exp_mass = jnp.sum(jnp.exp(logits - peak_value[:, None]), axis=1)
    column = vocab_start + jnp.arange(vocab_part, dtype=jnp.int32)
    target_logit = jnp.sum(
        jnp.where(column[None, :] == piece_targets[:, None], logits, 0.0), axis=1
    )
    from_peaks, from_masses, from_logits = sent_together(
        (
            peak_value.reshape(experts, token_count),
            exp_mass.reshape(experts, token_count),
            target_logit.reshape(experts, token_count),
        ),
        "expert",
        0,
        0,
        1,
    )
    peak_mine = jnp.max(from_peaks, axis=0)
    mass_mine = jnp.sum(from_masses * jnp.exp(from_peaks - peak_mine[None, :]), axis=0)
    logit_mine = jnp.sum(from_logits, axis=0)
    ref_logp = logit_mine - (peak_mine + jnp.log(mass_mine))
    log_ratio = jnp.clip(ref_logp - policy_logp.reshape(-1), -10.0, 10.0)
    token_value = jnp.exp(log_ratio) - log_ratio - 1.0
    position = lax.axis_index("expert") * pos_count + jnp.arange(pos_count, dtype=jnp.int32)
    inside = position[None, :] < owned_lengths[:, None]
    token_kl = jnp.where(inside, token_value.reshape(row_count, pos_count), 0.0)
    row_total = taken_together(jnp.sum(token_kl, axis=1), "expert")
    row_kl = row_total / owned_lengths.astype(jnp.float32)
    return (token_kl.reshape(1, row_count, pos_count), row_kl)


def solution(mesh):
    in_specs = (
        P("expert", "dp", None, None),
        P("dp"),
        P("dp"),
        P("expert", "dp", None, None),
        P("expert", "dp", None, None),
        P(),
        P("expert", None, "dp"),
        P("expert", None, "dp"),
        P("expert", "dp", None),
        P(),
        P(None, "expert"),
        P("expert", "dp", None),
        P("expert", "dp", None),
    )
    out_specs = (P("expert", "dp", None), P("dp"))
    return jax.shard_map(
        on_device, mesh=mesh, in_specs=in_specs, out_specs=out_specs, check_vma=False
    )
```

profile of v0, /device:TPU:1, one launch (start us, length us, event | category | flops | bytes accessed | tf_op | source)
XLA Modules:
  0.0 478.5 jit_solution(13261250315664766353)
XLA Ops:
  7.2 2.9 copy.42
  10.1 4.1 copy.41
  14.3 5.5 %pad_maximum_fusion = bf16[256,12288]{1,0:T(8,128)(2,1)} fusion(bf16[256,4096]{1,0:T(8,128)(2,1)} %bitcast.61, bf16[256,4096]{1,0:T(8,128)(2,1)S(1)} %bitcast.58, bf16[256,4096]{1,0:T(8,128)(2,1)} %bitcast.59), kind=kLoop, calls=%fused_computation.11 | loop fusion | flops 18874368 | bytes 12582912 | tf_op jit(solution)/shard_map/concatenate | solution.py:24
  19.8 0.6 copy-done.7
  20.4 0.6 broadcast_in_dim.25
  21.0 4.8 %all-to-all-start = ((s32[4,1,8]{2,1,0:T(1,128)}), s32[4,1,8]{2,1,0:T(1,128)S(1)}, u32[]{:S(2)}, u32[]{:S(2)}) async-start(s32[4,1,8]{2,1,0:T(1,128)} %broadcast_in_dim.25), calls=%async_computation | async-start | bytes 4096 | tf_op jit(solution)/shard_map/all_to_all | solution.py:15
  26.5 3.5 all-to-all-done
  30.0 1.3 broadcast_in_dim.54
  31.3 3.5 all-to-all-start.2
  35.0 0.5 broadcast.334
  35.5 0.7 reduce.11
  36.5 5.2 %all-to-all-done.2 = bf16[4,1,8,2,4096]{4,3,2,1,0:T(2,128)(2,1)S(1)} async-done(((bf16[4,1,8,2,4096]{4,3,2,1,0:T(2,128)(2,1)}), bf16[4,1,8,2,4096]{4,3,2,1,0:T(2,128)(2,1)S(1)}, u32[]{:S(2)}, u32[]{:S(2)}) %all-to-all-start.2) | async-done | bytes 524320 | tf_op jit(solution)/shard_map/all_to_all | solution.py:15
  41.7 1.6 scatter_fusion
  43.9 5.8 %scatter_custom_fusion.2 = bf16[256,4096]{1,0:T(8,128)(2,1)S(1)} fusion(s32[128]{0:T(128)S(1)} %fusion.31, bf16[16,4096]{1,0:T(8,128)(2,1)S(1)} %multiply_convert_fusion.1, s32[1024]{0:T(1024)S(1)} %pad_clamp_fusion.1, bf16[]{:T(256)} %constant.72.clone.1), kind=kCustom, calls=%fused_computation.19 | custom fusion | bytes 2097154 | tf_op jit(solution)/shard_map/scatter | solution.py:113
  49.6 2.2 reshape.361
  51.9 64.9 %all_to_all.45 = bf16[64,4,4096]{2,1,0:T(4,128)(2,1)S(1)} all-to-all(bf16[64,4,4096]{2,1,0:T(4,128)(2,1)} %reshape.361), channel_id=1, replica_groups=mesh['dp'=4,'expert'=64] {'expert'}, dimensions={0} | all-to-all | bytes 4194304 | tf_op jit(solution)/shard_map/all_to_all | solution.py:116
  116.7 2.1 reshape.362
  118.8 131.1 %all-gather.3.cloned.1.call-done = bf16[1024,12288]{1,0:T(8,128)(2,1)} async-done(((bf16[256,12288]{1,0:T(8,128)(2,1)}), bf16[1024,12288]{1,0:T(8,128)(2,1)}) %all-gather.3.cloned.1.call-update) | async-done | bytes 25165840 | tf_op jit(solution)/shard_map/all_gather | solution.py:25
  249.9 7.4 %fusion.3 = f32[256,1024]{1,0:T(8,128)} fusion(bf16[256,4096]{1,0:T(8,128)(2,1)} %reshape.362, bf16[1024,12288]{1,0:T(8,128)(2,1)} %all-gather.3.cloned.1.call-done), kind=kOutput, calls=%fused_computation.10 | convolution fusion | flops 2147483648 | bytes 11534336 | tf_op jit(solution)/shard_map/dot_general | solution.py:50
  257.3 12.1 %fusion.4 = bf16[256,4096]{1,0:T(8,128)(2,1)} fusion(bf16[1024,12288]{1,0:T(8,128)(2,1)} %all-gather.3.cloned.1.call-done, bf16[256,4096]{1,0:T(8,128)(2,1)S(1)} %copy-done, f32[256,1024]{1,0:T(8,128)} %fusion.3), kind=kOutput, calls=%fused_computation.12 | convolution fusion | flops 4297588736 | bytes 22020096 | tf_op jit(solution)/shard_map/dot_general | solution.py:53
  269.4 4.1 reshape.367
  273.5 11.0 %all-to-all-start.4 = ((bf16[64,4,4096]{2,1,0:T(4,128)(2,1)}), bf16[64,4,4096]{2,1,0:T(4,128)(2,1)}, u32[]{:S(2)}, u32[]{:S(2)}) async-start(bf16[64,4,4096]{2,1,0:T(4,128)(2,1)} %reshape.367), calls=%async_computation.4 | async-start | bytes 4194304 | tf_op jit(solution)/shard_map/all_to_all | solution.py:126
  284.6 0.6 pad_clamp_fusion
  285.2 49.0 %all-to-all-done.4 = bf16[64,4,4096]{2,1,0:T(4,128)(2,1)} async-done(((bf16[64,4,4096]{2,1,0:T(4,128)(2,1)}), bf16[64,4,4096]{2,1,0:T(4,128)(2,1)}, u32[]{:S(2)}, u32[]{:S(2)}) %all-to-all-start.4) | async-done | bytes 2097184 | tf_op jit(solution)/shard_map/all_to_all | solution.py:126
  334.2 2.5 reshape.368
  336.8 1.4 gather_fusion
  338.2 1.5 fusion.7
  339.9 0.3 multiply_reduce_fusion
  340.2 0.8 multiply_convert_fusion
  341.0 1.2 broadcast_in_dim.27
  342.2 3.5 all-to-all-start.1
  345.7 0.8 copy.43
  346.6 1.3 dynamic-slice
  348.5 0.2 dynamic-update-slice
  348.8 15.0 %all-reduce = s32[1024]{0:T(1024)S(1)} all-reduce(s32[1024]{0:T(1024)S(1)} %dynamic-update-slice), channel_id=1, replica_groups=mesh['dp'=4,'expert'=64] {'expert'}, use_global_device_ids=true, to_apply=%add | all-reduce | flops 1024 | bytes 8192
  363.8 57.9 %all-gather.5.cloned.1.call-done = bf16[1024,4096]{1,0:T(8,128)(2,1)} async-done(((bf16[16,4096]{1,0:T(8,128)(2,1)}), bf16[1024,4096]{1,0:T(8,128)(2,1)}) %all-gather.5.cloned.1.call-update) | async-done | bytes 8388624 | tf_op jit(solution)/shard_map/all_gather | solution.py:134
  421.6 15.1 %fusion.35 = (f32[1024]{0:T(1024)S(1)}, f32[1024,1024]{0,1:T(8,128)}) fusion(bf16[1024,4096]{1,0:T(8,128)(2,1)} %all-gather.5.cloned.1.call-done, bf16[4096,1024]{1,0:T(8,128)(2,1)} %param.23), kind=kOutput, calls=%fused_computation.82 | convolution fusion | flops 8590982144 | bytes 20975616 | tf_op jit(solution)/shard_map/dot_general | solution.py:136
  436.8 2.8 exponential_reduce_fusion
  439.8 0.7 pad_maximum_fusion.1
  440.5 5.8 %all-to-all-start.5 = ((f32[64,1,48]{2,1,0:T(1,128)}), f32[64,1,48]{2,1,0:T(1,128)S(1)}, u32[]{:S(2)}, u32[]{:S(2)}) async-start(f32[64,1,48]{2,1,0:T(1,128)} %bitcast.22), calls=%async_computation.5 | async-start | bytes 65536 | tf_op jit(solution)/shard_map/all_to_all | solution.py:36
  446.5 0.7 reduce.12
  447.2 0.8 scatter_custom_fusion
  448.0 7.7 %all-to-all-done.5 = f32[64,1,48]{2,1,0:T(1,128)S(1)} async-done(((f32[64,1,48]{2,1,0:T(1,128)}), f32[64,1,48]{2,1,0:T(1,128)S(1)}, u32[]{:S(2)}, u32[]{:S(2)}) %all-to-all-start.5) | async-done | bytes 12320 | tf_op jit(solution)/shard_map/all_to_all | solution.py:36
  456.2 0.6 broadcast_in_dim.59
  456.8 4.7 all-to-all-start.6
  461.6 0.6 copy.48
  462.3 8.8 %all-to-all-done.6 = f32[64,1,8]{2,1,0:T(1,128)S(1)} async-done(((f32[64,1,8]{2,1,0:T(1,128)}), f32[64,1,8]{2,1,0:T(1,128)S(1)}, u32[]{:S(2)}, u32[]{:S(2)}) %all-to-all-start.6) | async-done | bytes 2080 | tf_op jit(solution)/shard_map/all_to_all | solution.py:15
  471.1 0.5 convert_divide_fusion
  (63 shorter events, 3.2 us)
Async XLA Ops:
  7.2 242.7 %all-gather.3.cloned.1.call-start = ((), (), s32[]{:S(2)}) async-start(), calls=%async_computation.7 | async-start | bytes 31457280 | tf_op jit(solution)/shard_map/all_gather | solution.py:25
  19.8 0.7 copy-start.7
  19.8 6.1 %copy-start.2 = (s32[1,8,2,8]{3,2,1,0:T(2,128)S(1)}, s32[1,8,2,8]{3,2,1,0:T(2,128)}, u32[]{:S(2)}) copy-start(s32[1,8,2,8]{3,2,1,0:T(2,128)} %param.16) | copy-start | bytes 1540
  19.8 10.2 %copy-start.1 = (bf16[1,8,2,4096]{3,2,1,0:T(2,128)(2,1)S(1)}, bf16[1,8,2,4096]{3,2,1,0:T(2,128)(2,1)}, u32[]{:S(2)}) copy-start(bf16[1,8,2,4096]{3,2,1,0:T(2,128)(2,1)} %param.13) | copy-start | bytes 393220
  19.8 24.0 %copy-start.3 = (f32[4096]{0:T(1024)S(1)}, f32[4096]{0:T(1024)}, u32[]{:S(2)}) copy-start(f32[4096]{0:T(1024)} %param.18) | copy-start | bytes 49156
  21.0 9.0 %all-to-all-start = ((s32[4,1,8]{2,1,0:T(1,128)}), s32[4,1,8]{2,1,0:T(1,128)S(1)}, u32[]{:S(2)}, u32[]{:S(2)}) async-start(s32[4,1,8]{2,1,0:T(1,128)} %broadcast_in_dim.25), calls=%async_computation | async-start | bytes 4096 | tf_op jit(solution)/shard_map/all_to_all | solution.py:15
  31.3 10.4 %all-to-all-start.2 = ((bf16[4,1,8,2,4096]{4,3,2,1,0:T(2,128)(2,1)}), bf16[4,1,8,2,4096]{4,3,2,1,0:T(2,128)(2,1)S(1)}, u32[]{:S(2)}, u32[]{:S(2)}) async-start(bf16[4,1,8,2,4096]{4,3,2,1,0:T(2,128)(2,1)} %broadcast_in_dim.54), calls=%async_computation.2 | async-start | bytes 1048576 | tf_op jit(solution)/shard_map/all_to_all | solution.py:15
  36.5 6.9 %copy-start.6 = (s32[32]{0:T(128)}, s32[32]{0:T(128)S(1)}, u32[]{:S(2)}) copy-start(s32[32]{0:T(128)S(1)} %fusion.30) | copy-start | bytes 388
  118.8 138.5 %copy-start = (bf16[256,4096]{1,0:T(8,128)(2,1)S(1)}, bf16[256,4096]{1,0:T(8,128)(2,1)}, u32[]{:S(2)}) copy-start(bf16[256,4096]{1,0:T(8,128)(2,1)} %reshape.362) | copy-start | bytes 6291460
  273.5 60.7 %all-to-all-start.4 = ((bf16[64,4,4096]{2,1,0:T(4,128)(2,1)}), bf16[64,4,4096]{2,1,0:T(4,128)(2,1)}, u32[]{:S(2)}, u32[]{:S(2)}) async-start(bf16[64,4,4096]{2,1,0:T(4,128)(2,1)} %reshape.367), calls=%async_computation.4 | async-start | bytes 4194304 | tf_op jit(solution)/shard_map/all_to_all | solution.py:126
  284.6 137.1 %all-gather.5.cloned.1.call-start = ((), (), s32[]{:S(2)}) async-start(), calls=%async_computation.8 | async-start | bytes 8519680 | tf_op jit(solution)/shard_map/all_gather | solution.py:134
  336.7 3.5 copy-start.4
  342.2 98.3 %all-to-all-start.1 = ((s32[4,1,8]{2,1,0:T(1,128)}), s32[4,1,8]{2,1,0:T(1,128)S(1)}, u32[]{:S(2)}, u32[]{:S(2)}) async-start(s32[4,1,8]{2,1,0:T(1,128)} %broadcast_in_dim.27), calls=%async_computation.1 | async-start | bytes 4096 | tf_op jit(solution)/shard_map/all_to_all | solution.py:15
  436.7 9.6 %copy-start.5 = (f32[1,8,2]{1,2,0:T(2,128)S(1)}, f32[1,8,2]{1,2,0:T(2,128)}, u32[]{:S(2)}) copy-start(f32[1,8,2]{1,2,0:T(2,128)} %param.25) | copy-start | bytes 196
  440.5 15.2 %all-to-all-start.5 = ((f32[64,1,48]{2,1,0:T(1,128)}), f32[64,1,48]{2,1,0:T(1,128)S(1)}, u32[]{:S(2)}, u32[]{:S(2)}) async-start(f32[64,1,48]{2,1,0:T(1,128)} %bitcast.22), calls=%async_computation.5 | async-start | bytes 65536 | tf_op jit(solution)/shard_map/all_to_all | solution.py:36
  456.8 14.2 %all-to-all-start.6 = ((f32[64,1,8]{2,1,0:T(1,128)}), f32[64,1,8]{2,1,0:T(1,128)S(1)}, u32[]{:S(2)}, u32[]{:S(2)}) async-start(f32[64,1,8]{2,1,0:T(1,128)} %broadcast_in_dim.59), calls=%async_computation.6 | async-start | bytes 65536 | tf_op jit(solution)/shard_map/all_to_all | solution.py:15
Sparse Core Ops, SparseCore 0:
  19.9 229.9 all-gather.2
  341.1 80.4 all-gather.4
where the time goes:
time: 480 us; the launch traced here: 479 us
  waiting for transfers between devices  263 us (55%)
  blocking collectives  79.9 us (17%)
  local copies, waits for them, and re-layouts  36.9 us (8%)
  matrix products  34.6 us (7%)
  starting transfers between devices  33.4 us (7%)
  other arithmetic  15.6 us (3%)
  between operations  14.9 us (3%)
    all_gather x1, waiting for transfers between devices, gather_turned(): whole, at, done = (lax.all_gather(both, axis, axis=0, tiled=True), 0, [])  131 us
    all_to_all x1, blocking collectives, on_device(): lax.all_to_all(sender.reshape(experts, slot_bound, features), 'expert', s...  64.9 us
    all_gather x1, waiting for transfers between devices, on_device(): piece_rows = lax.all_gather(final_rows, 'expert', axis=0, tiled=True)  57.9 us
    all_to_all x1, waiting for transfers between devices, on_device(): lax.all_to_all(worked, 'expert', split_axis=0, concat_axis=0, tiled=True)  49 us
    all_to_all x4, waiting for transfers between devices, sent_to_all(): return lax.all_to_all(copies, axis, split_axis=0, concat_axis=0, tiled=True)  17.5 us
    all_to_all x4, starting transfers between devices, sent_to_all(): return lax.all_to_all(copies, axis, split_axis=0, concat_axis=0, tiled=True)  16.5 us
    dot_general x1, matrix products, on_device(): jnp.dot(piece_rows, head_weight, preferred_element_type=jnp.float32)  15.1 us
    unnamed x1, blocking collectives  15 us
  transfers between devices with their start and end apart: 8, of which 7 were waited for; matrix products, arithmetic and copies ran while one was open for 9% of the time, Pallas kernels for 0%

commit v1 on v0

--- a/solution.py
+++ b/solution.py
@@ -22,7 +22,13 @@
 def gather_turned(arrays, axis, dims):
     turned = [jnp.moveaxis(a, dim, 0) for a, dim in zip(arrays, dims)]
     both = jnp.concatenate([t.reshape(len(t), -1) for t in turned], axis=1)
-    whole, at, done = (lax.all_gather(both, axis, axis=0, tiled=True), 0, [])
+    whole, at, done = (
+        jnp.concatenate(
+            lax.all_to_all(jnp.stack([both] * lax.axis_size(axis)), axis, 0, 0), axis=0
+        ),
+        0,
+        [],
+    )
     for t, dim in zip(turned, dims):
         share = whole[:, at : at + t[0].size].reshape(-1, *t.shape[1:])
         done.append(jnp.moveaxis(share, 0, dim))

time: 480 us -> 623 us (1.30)
  waiting for transfers between devices: 263 us -> 434 us
  blocking collectives: 79.9 us -> 15.1 us
  starting transfers between devices: 33.4 us -> 55.1 us
  local copies, waits for them, and re-layouts: 36.9 us -> 50.4 us
    all_to_all x0 -> x2, waiting for transfers between devices: none -> 305 us  [the longest x1 269 us: gather_turned(): lax.all_to_all(jnp.stack([both] * lax.axis_size(axis)), axis, 0, 0)]
    all_gather x1 -> x0, waiting for transfers between devices: 131 us -> none  [gather_turned(): whole, at, done = (lax.all_gather(both, axis, axis=0, tiled=True), 0, [])]
    all_to_all x1 -> x0, blocking collectives: 64.9 us -> none  [on_device(): lax.all_to_all(sender.reshape(experts, slot_bound, features), 'expert', s...]
    all_to_all x0 -> x2, starting transfers between devices: none -> 23.8 us  [the longest x1 15.1 us: on_device(): lax.all_to_all(sender.reshape(experts, slot_bound, features), 'expert', s...]
    another operation x0 -> x1, local copies, waits for them, and re-layouts: none -> 10.8 us  [gather_turned(): jnp.stack([both] * lax.axis_size(axis))]
  transfers between devices with their start and end apart: 8 -> 9, of which waited for: 7 -> 8; matrix products, arithmetic and copies ran while one was open for 9% -> 7% of each run, Pallas kernels for 0% -> 0%
where the time goes in v1:
time: 623 us; the launch traced here: 622 us
  waiting for transfers between devices  434 us (70%)
  starting transfers between devices  55.1 us (9%)
  local copies, waits for them, and re-layouts  50.4 us (8%)
  matrix products  34.7 us (6%)
  other arithmetic  17.1 us (3%)
  blocking collectives  15.1 us (2%)
  between operations  15 us (2%)
    all_to_all x1, waiting for transfers between devices, gather_turned(): lax.all_to_all(jnp.stack([both] * lax.axis_size(axis)), axis, 0, 0)  269 us
    all_gather x1, waiting for transfers between devices, on_device(): piece_rows = lax.all_gather(final_rows, 'expert', axis=0, tiled=True)  56.9 us
    all_to_all x1, waiting for transfers between devices, on_device(): lax.all_to_all(worked, 'expert', split_axis=0, concat_axis=0, tiled=True)  49 us
    all_to_all x1, waiting for transfers between devices, on_device(): lax.all_to_all(sender.reshape(experts, slot_bound, features), 'expert', s...  35.2 us
    all_to_all x4, starting transfers between devices, sent_to_all(): return lax.all_to_all(copies, axis, split_axis=0, concat_axis=0, tiled=True)  16.2 us
    all_to_all x4, waiting for transfers between devices, sent_to_all(): return lax.all_to_all(copies, axis, split_axis=0, concat_axis=0, tiled=True)  16.1 us
    all_to_all x1, starting transfers between devices, on_device(): lax.all_to_all(sender.reshape(experts, slot_bound, features), 'expert', s...  15.1 us
    unnamed x1, blocking collectives  15.1 us
  transfers between devices with their start and end apart: 9, of which 8 were waited for; matrix products, arithmetic and copies ran while one was open for 7% of the time, Pallas kernels for 0%

profile of v1, /device:TPU:1, one launch (start us, length us, event | category | flops | bytes accessed | tf_op | source)
XLA Modules:
  0.0 621.5 jit_solution(8766128931211902057)
XLA Ops:
  7.2 1.3 broadcast_in_dim.25
  8.4 4.8 all-to-all-start
  13.3 0.7 broadcast_multiply_fusion
  14.0 0.8 eq.61
  15.3 2.1 all-to-all-done
  17.4 2.2 broadcast_in_dim.54
  19.6 3.5 all-to-all-start.2
  23.8 0.7 reduce.11
  24.7 5.2 all-to-all-done.2
  30.0 1.6 scatter_fusion
  32.1 5.8 scatter_custom_fusion.2
  37.9 2.2 reshape.366
  40.1 15.1 %all-to-all-start.3 = ((bf16[64,4,4096]{2,1,0:T(4,128)(2,1)}), bf16[64,4,4096]{2,1,0:T(4,128)(2,1)S(1)}, u32[]{:S(2)}, u32[]{:S(2)}) async-start(bf16[64,4,4096]{2,1,0:T(4,128)(2,1)} %reshape.366), calls=%async_computation.3 | async-start | bytes 4194304 | tf_op jit(solution)/shard_map/all_to_all | solution.py:122
  55.3 4.1 copy.42
  59.4 4.1 copy.41
  63.5 6.3 %pad_maximum_fusion = bf16[256,12288]{1,0:T(8,128)(2,1)} fusion(bf16[256,4096]{1,0:T(8,128)(2,1)} %bitcast.62, bf16[256,4096]{1,0:T(8,128)(2,1)} %bitcast.59, bf16[256,4096]{1,0:T(8,128)(2,1)} %bitcast.60), kind=kLoop, calls=%fused_computation.11 | loop fusion | flops 18874368 | bytes 12582912 | tf_op jit(solution)/shard_map/concatenate | solution.py:24
  69.8 35.2 %all-to-all-done.3 = bf16[64,4,4096]{2,1,0:T(4,128)(2,1)S(1)} async-done(((bf16[64,4,4096]{2,1,0:T(4,128)(2,1)}), bf16[64,4,4096]{2,1,0:T(4,128)(2,1)S(1)}, u32[]{:S(2)}, u32[]{:S(2)}) %all-to-all-start.3) | async-done | bytes 2097184 | tf_op jit(solution)/shard_map/all_to_all | solution.py:122
  105.0 10.8 %stack.2 = bf16[4,256,12288]{2,1,0:T(8,128)(2,1)} broadcast(bf16[256,12288]{1,0:T(8,128)(2,1)} %pad_maximum_fusion), dimensions={1,2} | broadcast | bytes 31457280 | tf_op jit(solution)/shard_map/stack | solution.py:27
  115.7 8.6 %all-to-all-start.4 = ((bf16[4,256,12288]{2,1,0:T(8,128)(2,1)}), bf16[4,256,12288]{2,1,0:T(8,128)(2,1)}, u32[]{:S(2)}, u32[]{:S(2)}) async-start(bf16[4,256,12288]{2,1,0:T(8,128)(2,1)} %stack.2), calls=%async_computation.4 | async-start | bytes 50331648 | tf_op jit(solution)/shard_map/all_to_all | solution.py:27
  124.4 2.0 reshape.367
  126.4 269.4 %all-to-all-done.4 = bf16[4,256,12288]{2,1,0:T(8,128)(2,1)} async-done(((bf16[4,256,12288]{2,1,0:T(8,128)(2,1)}), bf16[4,256,12288]{2,1,0:T(8,128)(2,1)}, u32[]{:S(2)}, u32[]{:S(2)}) %all-to-all-start.4) | async-done | bytes 25165856 | tf_op jit(solution)/shard_map/all_to_all | solution.py:27
  395.8 7.5 %fusion.3 = f32[256,1024]{1,0:T(8,128)} fusion(bf16[256,4096]{1,0:T(8,128)(2,1)} %reshape.367, bf16[1024,12288]{1,0:T(8,128)(2,1)} %bitcast.13), kind=kOutput, calls=%fused_computation.10 | convolution fusion | flops 2147483648 | bytes 11534336 | tf_op jit(solution)/shard_map/dot_general | solution.py:56
  403.3 12.1 %fusion.4 = bf16[256,4096]{1,0:T(8,128)(2,1)} fusion(bf16[1024,12288]{1,0:T(8,128)(2,1)} %bitcast.13, bf16[256,4096]{1,0:T(8,128)(2,1)S(1)} %copy-done, f32[256,1024]{1,0:T(8,128)} %fusion.3), kind=kOutput, calls=%fused_computation.12 | convolution fusion | flops 4297588736 | bytes 22020096 | tf_op jit(solution)/shard_map/dot_general | solution.py:59
  415.4 4.1 reshape.373
  419.5 9.3 %all-to-all-start.5 = ((bf16[64,4,4096]{2,1,0:T(4,128)(2,1)}), bf16[64,4,4096]{2,1,0:T(4,128)(2,1)}, u32[]{:S(2)}, u32[]{:S(2)}) async-start(bf16[64,4,4096]{2,1,0:T(4,128)(2,1)} %reshape.373), calls=%async_computation.5 | async-start | bytes 4194304 | tf_op jit(solution)/shard_map/all_to_all | solution.py:132
  428.9 0.6 pad_clamp_fusion
  429.5 49.0 %all-to-all-done.5 = bf16[64,4,4096]{2,1,0:T(4,128)(2,1)} async-done(((bf16[64,4,4096]{2,1,0:T(4,128)(2,1)}), bf16[64,4,4096]{2,1,0:T(4,128)(2,1)}, u32[]{:S(2)}, u32[]{:S(2)}) %all-to-all-start.5) | async-done | bytes 2097184 | tf_op jit(solution)/shard_map/all_to_all | solution.py:132
  478.4 2.5 reshape.374
  481.0 1.4 gather_fusion
  482.5 1.5 fusion.7
  484.5 0.8 multiply_convert_fusion
  485.2 1.2 broadcast_in_dim.27
  486.5 3.2 all-to-all-start.1
  489.7 0.8 copy.43
  490.5 1.3 dynamic-slice
  492.7 15.1 %all-reduce = s32[1024]{0:T(1024)S(1)} all-reduce(s32[1024]{0:T(1024)S(1)} %dynamic-update-slice), channel_id=1, replica_groups=mesh['dp'=4,'expert'=64] {'expert'}, use_global_device_ids=true, to_apply=%add | all-reduce | flops 1024 | bytes 8192
  507.8 56.9 %all-gather.2.cloned.1.call-done = bf16[1024,4096]{1,0:T(8,128)(2,1)} async-done(((bf16[16,4096]{1,0:T(8,128)(2,1)}), bf16[1024,4096]{1,0:T(8,128)(2,1)}) %all-gather.2.cloned.1.call-update) | async-done | bytes 8388624 | tf_op jit(solution)/shard_map/all_gather | solution.py:140
  564.7 15.1 %fusion.35 = (f32[1024]{0:T(1024)S(1)}, f32[1024,1024]{0,1:T(8,128)}) fusion(bf16[1024,4096]{1,0:T(8,128)(2,1)} %all-gather.2.cloned.1.call-done, bf16[4096,1024]{1,0:T(8,128)(2,1)} %param.23), kind=kOutput, calls=%fused_computation.82 | convolution fusion | flops 8590982144 | bytes 20975616 | tf_op jit(solution)/shard_map/dot_general | solution.py:142
  579.9 2.8 exponential_reduce_fusion
  582.9 0.7 pad_maximum_fusion.1
  583.6 5.8 all-to-all-start.6
  589.5 0.7 reduce.12
  590.3 0.8 scatter_custom_fusion
  591.1 7.7 %all-to-all-done.6 = f32[64,1,48]{2,1,0:T(1,128)S(1)} async-done(((f32[64,1,48]{2,1,0:T(1,128)}), f32[64,1,48]{2,1,0:T(1,128)S(1)}, u32[]{:S(2)}, u32[]{:S(2)}) %all-to-all-start.6) | async-done | bytes 12320 | tf_op jit(solution)/shard_map/all_to_all | solution.py:42
  599.2 0.6 broadcast_in_dim.59
  599.9 4.7 all-to-all-start.7
  604.6 0.6 copy.48
  605.3 8.8 %all-to-all-done.7 = f32[64,1,8]{2,1,0:T(1,128)S(1)} async-done(((f32[64,1,8]{2,1,0:T(1,128)}), f32[64,1,8]{2,1,0:T(1,128)S(1)}, u32[]{:S(2)}, u32[]{:S(2)}) %all-to-all-start.7) | async-done | bytes 2080 | tf_op jit(solution)/shard_map/all_to_all | solution.py:15
  (58 shorter events, 4.6 us)
Async XLA Ops:
  7.2 24.8 %copy-start.1 = (f32[4096]{0:T(1024)S(1)}, f32[4096]{0:T(1024)}, u32[]{:S(2)}) copy-start(f32[4096]{0:T(1024)} %param.18) | copy-start | bytes 49156
  8.4 9.0 %all-to-all-start = ((s32[4,1,8]{2,1,0:T(1,128)}), s32[4,1,8]{2,1,0:T(1,128)S(1)}, u32[]{:S(2)}, u32[]{:S(2)}) async-start(s32[4,1,8]{2,1,0:T(1,128)} %broadcast_in_dim.25), calls=%async_computation | async-start | bytes 4096 | tf_op jit(solution)/shard_map/all_to_all | solution.py:15
  19.6 10.4 %all-to-all-start.2 = ((bf16[4,1,8,2,4096]{4,3,2,1,0:T(2,128)(2,1)}), bf16[4,1,8,2,4096]{4,3,2,1,0:T(2,128)(2,1)S(1)}, u32[]{:S(2)}, u32[]{:S(2)}) async-start(bf16[4,1,8,2,4096]{4,3,2,1,0:T(2,128)(2,1)} %broadcast_in_dim.54), calls=%async_computation.2 | async-start | bytes 1048576 | tf_op jit(solution)/shard_map/all_to_all | solution.py:15
  24.7 6.9 %copy-start.4 = (s32[32]{0:T(128)}, s32[32]{0:T(128)S(1)}, u32[]{:S(2)}) copy-start(s32[32]{0:T(128)S(1)} %fusion.30) | copy-start | bytes 388
  40.1 64.9 %all-to-all-start.3 = ((bf16[64,4,4096]{2,1,0:T(4,128)(2,1)}), bf16[64,4,4096]{2,1,0:T(4,128)(2,1)S(1)}, u32[]{:S(2)}, u32[]{:S(2)}) async-start(bf16[64,4,4096]{2,1,0:T(4,128)(2,1)} %reshape.366), calls=%async_computation.3 | async-start | bytes 4194304 | tf_op jit(solution)/shard_map/all_to_all | solution.py:122
  115.7 280.0 %all-to-all-start.4 = ((bf16[4,256,12288]{2,1,0:T(8,128)(2,1)}), bf16[4,256,12288]{2,1,0:T(8,128)(2,1)}, u32[]{:S(2)}, u32[]{:S(2)}) async-start(bf16[4,256,12288]{2,1,0:T(8,128)(2,1)} %stack.2), calls=%async_computation.4 | async-start | bytes 50331648 | tf_op jit(solution)/shard_map/all_to_all | solution.py:27
  395.8 7.5 %copy-start = (bf16[256,4096]{1,0:T(8,128)(2,1)S(1)}, bf16[256,4096]{1,0:T(8,128)(2,1)}, u32[]{:S(2)}) copy-start(bf16[256,4096]{1,0:T(8,128)(2,1)} %reshape.367) | copy-start | bytes 6291460
  419.5 58.9 %all-to-all-start.5 = ((bf16[64,4,4096]{2,1,0:T(4,128)(2,1)}), bf16[64,4,4096]{2,1,0:T(4,128)(2,1)}, u32[]{:S(2)}, u32[]{:S(2)}) async-start(bf16[64,4,4096]{2,1,0:T(4,128)(2,1)} %reshape.373), calls=%async_computation.5 | async-start | bytes 4194304 | tf_op jit(solution)/shard_map/all_to_all | solution.py:132
  428.8 135.9 %all-gather.2.cloned.1.call-start = ((), (), s32[]{:S(2)}) async-start(), calls=%async_computation.8 | async-start | bytes 8519680 | tf_op jit(solution)/shard_map/all_gather | solution.py:140
  481.0 3.5 copy-start.2
  486.5 97.1 %all-to-all-start.1 = ((s32[4,1,8]{2,1,0:T(1,128)}), s32[4,1,8]{2,1,0:T(1,128)S(1)}, u32[]{:S(2)}, u32[]{:S(2)}) async-start(s32[4,1,8]{2,1,0:T(1,128)} %broadcast_in_dim.27), calls=%async_computation.1 | async-start | bytes 4096 | tf_op jit(solution)/shard_map/all_to_all | solution.py:15
  579.8 9.6 %copy-start.3 = (f32[1,8,2]{1,2,0:T(2,128)S(1)}, f32[1,8,2]{1,2,0:T(2,128)}, u32[]{:S(2)}) copy-start(f32[1,8,2]{1,2,0:T(2,128)} %param.25) | copy-start | bytes 196
  583.6 15.2 %all-to-all-start.6 = ((f32[64,1,48]{2,1,0:T(1,128)}), f32[64,1,48]{2,1,0:T(1,128)S(1)}, u32[]{:S(2)}, u32[]{:S(2)}) async-start(f32[64,1,48]{2,1,0:T(1,128)} %bitcast.23), calls=%async_computation.6 | async-start | bytes 65536 | tf_op jit(solution)/shard_map/all_to_all | solution.py:42
  599.9 14.2 %all-to-all-start.7 = ((f32[64,1,8]{2,1,0:T(1,128)}), f32[64,1,8]{2,1,0:T(1,128)S(1)}, u32[]{:S(2)}, u32[]{:S(2)}) async-start(f32[64,1,8]{2,1,0:T(1,128)} %broadcast_in_dim.59), calls=%async_computation.7 | async-start | bytes 65536 | tf_op jit(solution)/shard_map/all_to_all | solution.py:15
Sparse Core Ops, SparseCore 0:
  485.4 79.2 all-gather.1
